TPU v7x, 32 devices: a whole 2x2x4 slice. The times are simulated.
32 devices in a mesh: ep: 4 (over y, core), fsdp: 8 (over z, x).
Axes of the slice: x: 2, y: 2, z: 4, core: 2. Of those that a mesh axis runs over, the one named last changes fastest.
Arguments:
- w_down: float32 [16, 6400, 4096], P('ep', None, 'fsdp'), may hold values from -0.109375 to 0.109375
- router_weight: float32 [4096, 16], P('fsdp', 'ep'), may hold values from -0.09375 to 0.09375
- router_gain: float32 [4096], P('fsdp'), may hold values from 0.25 to 1.75
Outputs:
- serve_down: bfloat16 [16, 6400, 4096], P('ep', 'fsdp')
- scale_down: float32 [16, 6400], P('ep', 'fsdp')
- serve_router: bfloat16 [4096, 16], replicated
All inputs are finite; a program needn't handle non-finite values.
Results may differ from a plain program's by a relative error of at most 0.001.
Values may be sent and summed in bfloat16 or wider, within the bound.
A program may use at most 192 MiB of HBM per device.

v0:
```python
import functools

import jax
import jax.numpy as jnp
from jax import lax
from jax.experimental import pallas as pl
from jax.experimental.pallas import tpu as pltpu
from jax.sharding import PartitionSpec as P

LANES = 128
MESH = pl.DeviceIdType.MESH


def target(me, j, n):
    return (me + j + 1) % n


def kernel(n, w, o, sc, xbuf, sbuf, part, recvp, mine, scales,
           load_sem, send_sem, recv_sem, psend, precv, ssend, srecv, own_sem):
    experts, rows, cols = w.shape
    block = rows // n
    tiles = -(-block // LANES)
    padded = part.shape[2]
    starts = [min(t * LANES, block - LANES) for t in range(tiles)]
    steps = n * experts
    slots = xbuf.shape[0]
    me = lax.axis_index("fsdp")

    def where(i):
        return target(me, i // experts, n), i % experts

    def load(i):
        d, e = where(i)
        s = i % slots
        return pltpu.make_async_copy(
            w.at[e, pl.ds(pl.multiple_of(d * block, 8), block), :], xbuf.at[s], load_sem.at[s])

    def peer(j):
        return target(me, j, n)

    def sums(to, source):
        return pltpu.make_async_remote_copy(
            src_ref=part.at[to], dst_ref=recvp.at[source], send_sem=psend.at[to],
            recv_sem=precv.at[source], device_id={"fsdp": to}, device_id_type=MESH)

    def scale_copy(to, source):
        return pltpu.make_async_remote_copy(
            src_ref=mine, dst_ref=scales.at[source], send_sem=ssend.at[to],
            recv_sem=srecv.at[source], device_id={"fsdp": to}, device_id_type=MESH)

    def bulk(i, to, e, source):
        return pltpu.make_async_remote_copy(
            src_ref=sbuf.at[i],
            dst_ref=o.at[e, :, pl.ds(pl.multiple_of(source * cols, LANES), cols)],
            send_sem=send_sem.at[i], recv_sem=recv_sem.at[source * experts + e],
            device_id={"fsdp": to}, device_id_type=MESH)

    def local(i, e):
        return pltpu.make_async_copy(
            sbuf.at[i], o.at[e, :, pl.ds(pl.multiple_of(me * cols, LANES), cols)], own_sem.at[e])

    def each(count, f):
        def step(i, c):
            f(i)
            return c
        lax.fori_loop(0, count, step, 0)

    each(slots, lambda k: load(steps - 1 - k).start())

    barrier = pltpu.get_barrier_semaphore()
    each(n - 1, lambda j: pl.semaphore_signal(
        barrier, inc=1, device_id={"fsdp": peer(j)}, device_id_type=MESH))
    pl.semaphore_wait(barrier, n - 1)

    def first(k):
        i = steps - 1 - k
        d, e = where(i)
        s = i % slots
        load(i).wait()
        found = []
        for start in starts:
            x = xbuf[s, start:start + LANES, :]
            y = x * x
            acc = y[:, :LANES]
            for c in range(LANES, cols, LANES):
                acc = acc + y[:, c:c + LANES]
            found.append(jnp.sum(acc.T, axis=0, keepdims=True))
        if padded > tiles:
            found.append(jnp.zeros((padded - tiles, LANES), jnp.float32))
        part[d, e] = jnp.concatenate(found, axis=0)

        @pl.when(i >= slots)
        def _():
            load(i - slots).start()

        @pl.when((e == 0) & (i // experts < n - 1))
        def _():
            sums(d, me).start()

    each(steps, first)

    def add(j, total):
        source = peer(j)
        sums(source, source).wait_recv()
        return total + recvp[source]

    total = lax.fori_loop(0, n - 1, add, part[me])
    scale = jnp.sqrt(total)
    sc[...] = scale
    mine[...] = scale
    scales[me] = scale
    each(n - 1, lambda j: scale_copy(peer(j), me).start())

    def second(i):
        d, e = where(i)
        s = i % slots

        @pl.when((e == 0) & (i // experts < n - 1))
        def _():
            scale_copy(d, d).wait_recv()

        @pl.when(i >= slots)
        def _():
            load(i).wait()

        inverse = 1.0 / scales[d, e]
        for t, start in enumerate(starts):
            factor = jnp.broadcast_to(inverse[t:t + 1, :], (LANES, LANES)).T
            for c in range(0, cols, LANES):
                x = xbuf[s, start:start + LANES, c:c + LANES]
                sbuf[i, start:start + LANES, c:c + LANES] = (x * factor).astype(jnp.bfloat16)

        @pl.when(i + slots < steps)
        def _():
            load(i + slots).start()

        @pl.when(i // experts < n - 1)
        def _():
            bulk(i, d, e, me).start()

        @pl.when(i // experts == n - 1)
        def _():
            local(i, e).start()

    each(steps, second)

    def drain(i):
        d, e = where(i)
        bulk(i, d, e, me).wait_send()
        bulk(i, d, e, d).wait_recv()

    def finish(j):
        sums(peer(j), me).wait_send()
        scale_copy(peer(j), me).wait_send()

    each(n - 1, finish)
    each(experts, lambda e: local(steps - experts + e, e).wait())
    each(steps - experts, drain)


def exchange(n, w):
    experts, rows, cols = w.shape
    block = rows // n
    tiles = -(-block // LANES)
    padded = -(-tiles // 8) * 8
    steps = n * experts
    slots = min(2 * n, steps)
    sums = (n, experts, padded, LANES)
    dma = pltpu.SemaphoreType.DMA
    o, sc = pl.pallas_call(
        functools.partial(kernel, n),
        out_shape=(
            jax.ShapeDtypeStruct((experts, block, n * cols), jnp.bfloat16),
            jax.ShapeDtypeStruct((experts, padded, LANES), jnp.float32),
        ),
        in_specs=[pl.BlockSpec(memory_space=pl.ANY)],
        out_specs=(pl.BlockSpec(memory_space=pl.ANY), pl.BlockSpec(memory_space=pltpu.VMEM)),
        scratch_shapes=[
            pltpu.VMEM((slots, block, cols), jnp.float32),
            pltpu.VMEM((steps, block, cols), jnp.bfloat16),
            pltpu.VMEM(sums, jnp.float32),
            pltpu.VMEM(sums, jnp.float32),
            pltpu.VMEM(sums[1:], jnp.float32),
            pltpu.VMEM(sums, jnp.float32),
            dma((slots,)), dma((steps,)), dma((steps,)),
            dma((n,)), dma((n,)), dma((n,)), dma((n,)), dma((experts,)),
        ],
        compiler_params=pltpu.CompilerParams(
            collective_id=0, has_side_effects=True, vmem_limit_bytes=58 * 1024 * 1024),
    )(w)
    tail = block - (tiles - 1) * LANES
    scale = jnp.concatenate(
        [sc[:, :tiles - 1].reshape(experts, (tiles - 1) * LANES), sc[:, tiles - 1, LANES - tail:]], axis=1)
    return o, scale


def body(n, w_down, router_weight, router_gain):
    serve_down, scale_down = exchange(n, w_down)
    part_router = (router_weight * router_gain[:, None]).astype(jnp.bfloat16)
    row_router = lax.all_gather(part_router, "fsdp", axis=0, tiled=True)
    serve_router = lax.all_gather(row_router, "ep", axis=1, tiled=True)
    return (serve_down, scale_down, serve_router)


def solution(mesh):
    in_specs = (P("ep", None, "fsdp"), P("fsdp", "ep"), P("fsdp"))
    out_specs = (P("ep", "fsdp", None), P("ep", "fsdp"), P())
    return jax.shard_map(
        functools.partial(body, mesh.shape["fsdp"]), mesh=mesh,
        in_specs=in_specs, out_specs=out_specs, check_vma=False)
```

profile of v0, /device:TPU:0, one launch (start us, length us, event | category | flops | bytes accessed | tf_op | source)
XLA Modules:
  0.0 646.6 jit_solution(9984306392826423086)
XLA Ops:
  0.6 0.0 copy-start
  0.6 0.0 copy-start.1
  0.7 449.1 %shard_map.58 = (bf16[4,800,4096]{2,1,0:T(8,128)(2,1)}, f32[4,8,128]{2,1,0:T(8,128)}) custom-call(f32[4,6400,512]{2,1,0:T(8,128)} %w.1), custom_call_target="tpu_custom_call" | custom-call | tf_op jit(solution)/shard_map/pallas_call | solution.py:170
  449.8 0.7 slice_bitcast_fusion
  450.5 0.8 slice.7
  451.3 0.6 pad_maximum_fusion
  451.9 0.0 copy-done
  451.9 0.0 copy-done.1
  451.9 170.7 %all_gather.6 = bf16[4096,4]{0,1:T(4,128)(2,1)S(1)} all-gather(bf16[512,4]{0,1:T(4,128)(2,1)S(1)} %multiply_convert_fusion), channel_id=1, replica_groups=mesh['ep'=4,'fsdp'=8] {'fsdp'}, dimensions={0}, use_global_device_ids=true | all-gather | bytes 36864 | tf_op jit(solution)/shard_map/all_gather | solution.py:200
  622.6 5.4 all-gather
  628.0 0.7 reshape.12
  628.7 17.9 %copy.10 = bf16[4,800,4096]{2,1,0:T(8,128)(2,1)} copy(bf16[4,800,4096]{2,1,0:T(8,128)(2,1)} %get-tuple-element.10) | data formatting | bytes 52428800
  (2 shorter events, 0.0 us)
Async XLA Ops:
  0.6 451.3 %copy-start = (f32[512,4]{0,1:T(4,128)S(1)}, f32[512,4]{0,1:T(4,128)}, u32[]{:S(2)}) copy-start(f32[512,4]{0,1:T(4,128)} %param.4) | copy-start | bytes 24580
  0.6 451.3 %copy-start.1 = (f32[512]{0:T(512)S(1)}, f32[512]{0:T(512)}, u32[]{:S(2)}) copy-start(f32[512]{0:T(512)} %param.5) | copy-start | bytes 6148
where the time goes:
time: 647 us
  Pallas kernels  449 us (69%)
  blocking collectives  176 us (27%)
  local copies, waits for them, and re-layouts  20.1 us (3%)
    pallas_call x1, Pallas kernels, exchange(): pl.pallas_call(functools.partial(kernel, n), out_shape=(jax.ShapeDtypeStr...  449 us
    all_gather x1, blocking collectives, body(): row_router = lax.all_gather(part_router, 'fsdp', axis=0, tiled=True)  171 us
    unnamed x8, local copies, waits for them, and re-layouts  19.4 us

commit v1 on v0

v1 whole, which is shorter than its diff:
```python
import functools

import jax
import jax.numpy as jnp
from jax import lax
from jax.experimental import pallas as pl
from jax.experimental.pallas import tpu as pltpu
from jax.sharding import PartitionSpec as P

LANES = 128
MESH = pl.DeviceIdType.MESH


def each(count, f):
    def step(i, c):
        f(i)
        return c
    lax.fori_loop(0, count, step, 0)


def ceil_to(a, b):
    return -(-a // b) * b


def kernel(n, m, w, rw, gain, o, sc, router,
           xbuf, sbuf, own, early, early_inv, part, recvp, mine, scales,
           rw_v, gain_v, rbuf, rwide, router_v, sc_v, sc_rows,
           load_a, load_b, arg_sem, esend, erecv, psend, precv, ssend, srecv,
           asend, arecv, bsend, brecv, own_sem, rsend, rrecv, gsend, grecv, out_sem):
    experts, rows, cols = w.shape
    block = rows // n
    tiles = -(-block // LANES)
    padded = part.shape[2]
    head = min(LANES, block)
    rest = block - head
    half = n // 2
    me = lax.axis_index("fsdp")
    group = lax.axis_index("ep")
    side = me // half
    mycols = pl.ds(pl.multiple_of(me * cols, LANES), cols)

    def peer(j):
        c = j // half
        return ((1 - side) * (1 - c) + side * c) * half + (me + j + c) % half

    def mate(j):
        return (group + j + 1) % m

    def send(src, dst, s, r, **to):
        return pltpu.make_async_remote_copy(
            src_ref=src, dst_ref=dst, send_sem=s, recv_sem=r,
            device_id=to, device_id_type=MESH)

    def load_head(d):
        return pltpu.make_async_copy(
            w.at[0, pl.ds(pl.multiple_of(d * block, 8), head), :],
            xbuf.at[d, pl.ds(0, head), :], load_a.at[d])

    def load_rest(d):
        return pltpu.make_async_copy(
            w.at[0, pl.ds(pl.multiple_of(d * block + head, 8), rest), :],
            xbuf.at[d, pl.ds(head, rest), :], load_b.at[d])

    def load(e, d):
        return pltpu.make_async_copy(
            w.at[e, pl.ds(pl.multiple_of(d * block, 8), block), :], xbuf.at[d], load_b.at[d])

    def early_copy(to, source):
        return send(early.at[me], early.at[source], esend.at[to], erecv.at[source], fsdp=to)

    def sums(e, to, source):
        return send(part.at[e, to], recvp.at[e, source],
                    psend.at[e, to], precv.at[e, source], fsdp=to)

    def scale_copy(e, to, source):
        return send(mine.at[e], scales.at[e, source],
                    ssend.at[e, to], srecv.at[e, source], fsdp=to)

    def bulk_head(j, to, source):
        return send(sbuf.at[0, j, pl.ds(0, head), :],
                    o.at[0, pl.ds(0, head), pl.ds(pl.multiple_of(source * cols, LANES), cols)],
                    asend.at[j], arecv.at[source], fsdp=to)

    def bulk_rest(j, to, source):
        return send(sbuf.at[0, j, pl.ds(head, rest), :],
                    o.at[0, pl.ds(head, rest), pl.ds(pl.multiple_of(source * cols, LANES), cols)],
                    bsend.at[0, j], brecv.at[0, source], fsdp=to)

    def bulk(e, j, to, source):
        return send(sbuf.at[e, j],
                    o.at[e, :, pl.ds(pl.multiple_of(source * cols, LANES), cols)],
                    bsend.at[e, j], brecv.at[e, source], fsdp=to)

    def local(e):
        return pltpu.make_async_copy(own.at[e % 2], o.at[e, :, mycols], own_sem.at[e % 2])

    width = rw.shape[1]
    rcols = width

    def router_copy(to, source):
        where = pl.ds(pl.multiple_of(source * rcols, LANES), rcols)
        return send(rbuf.at[group, :, where], rbuf.at[group, :, where],
                    rsend.at[to], rrecv.at[source], fsdp=to)

    def group_copy(to, source):
        return send(rbuf.at[source], rbuf.at[source], gsend.at[to], grecv.at[source], ep=to)

    get_rw = pltpu.make_async_copy(rw, rw_v, arg_sem.at[0])
    get_gain = pltpu.make_async_copy(gain, gain_v, arg_sem.at[1])

    barrier = pltpu.get_barrier_semaphore()
    each(n - 1, lambda j: pl.semaphore_signal(
        barrier, inc=1, device_id={"fsdp": peer(j)}, device_id_type=MESH))
    each(m - 1, lambda j: pl.semaphore_signal(
        barrier, inc=1, device_id={"ep": mate(j)}, device_id_type=MESH))

    each(n, lambda d: load_head(d).start())
    get_rw.start()
    get_gain.start()
    if rest:
        each(n, lambda d: load_rest(d).start())

    def row_sums(d, start, count):
        x = xbuf[d, start:start + count, :]
        y = x * x
        acc = y[:, :LANES]
        for c in range(LANES, cols, LANES):
            acc = acc + y[:, c:c + LANES]
        if count < LANES:
            acc = jnp.concatenate([acc, jnp.zeros((LANES - count, LANES), jnp.float32)], axis=0)
        return jnp.sum(acc.T, axis=0, keepdims=True)

    def scaled(d, inverse, start, count, store):
        factor = jnp.broadcast_to(inverse, (LANES, LANES)).T[:count]
        for c in range(0, cols, LANES):
            x = xbuf[d, start:start + count, c:c + LANES]
            store(start, count, c, (x * factor).astype(jnp.bfloat16))

    spans = [(t, t * LANES, min(LANES, block - t * LANES)) for t in range(tiles)]
    late = [span for span in spans if span[1] >= head]

    def begin(d):
        load_head(d).wait()
        early[me, pl.ds(d, 1), :] = row_sums(d, 0, head)

    each(n, begin)

    pl.semaphore_wait(barrier, n - 1 + m - 1)
    each(n - 1, lambda j: early_copy(peer(j), me).start())

    get_rw.wait()
    get_gain.wait()
    rbuf[group, :, pl.ds(pl.multiple_of(me * rcols, LANES), rcols)] = (
        rw_v[...] * gain_v[...]).astype(jnp.bfloat16)

    each(n - 1, lambda j: early_copy(peer(j), peer(j)).wait_recv())
    early_total = early[0]
    for s in range(1, n):
        early_total = early_total + early[s]
    early_inv[0] = 1.0 / jnp.sqrt(early_total)
    early_inv[1] = early_total

    def send_head(j):
        d = peer(j)

        def store(start, count, c, value):
            sbuf[0, j, start:start + count, c:c + LANES] = value

        scaled(d, early_inv[0, pl.ds(d, 1), :], 0, head, store)
        bulk_head(j, d, me).start()

    each(n - 1, send_head)
    each(n - 1, lambda j: router_copy(peer(j), me).start())

    def partial(e, d, which):
        found = [jnp.zeros((1, LANES), jnp.float32)] * (tiles - len(which))
        found += [row_sums(d, start, count) for _, start, count in which]
        if padded > tiles:
            found.append(jnp.zeros((padded - tiles, LANES), jnp.float32))
        part[e, d] = jnp.concatenate(found, axis=0)

    def add_up(e):
        def add(j, total):
            source = peer(j)
            sums(e, source, source).wait_recv()
            return total + recvp[e, source]

        return lax.fori_loop(0, n - 1, add, part[e, me])

    def publish(e, total):
        scale = jnp.sqrt(total)
        inverse = 1.0 / scale
        mine[e] = inverse
        scales[e, me] = inverse
        for t, start, count in spans:
            sc_rows[e, :, start:start + count] = scale[t:t + 1, :count]
        each(n - 1, lambda j: scale_copy(e, peer(j), me).start())

    def keep(e):
        def store(start, count, c, value):
            own[e % 2, start:start + count, c:c + LANES] = value

        inverse = scales[e, me]
        for t, start, count in spans:
            scaled(me, inverse[t:t + 1, :], start, count, store)
        local(e).start()

    def spread(e, j, which):
        d = peer(j)
        scale_copy(e, d, d).wait_recv()

        def store(start, count, c, value):
            sbuf[e, j, start:start + count, c:c + LANES] = value

        inverse = scales[e, d]
        for t, start, count in which:
            scaled(d, inverse[t:t + 1, :], start, count, store)

    def first_sums(j):
        d = peer(j)
        if rest:
            load_rest(d).wait()
        partial(0, d, late)
        sums(0, d, me).start()

    each(n - 1, first_sums)
    if rest:
        load_rest(me).wait()
    partial(0, me, late)
    total = add_up(0)
    first_row = lax.broadcasted_iota(jnp.int32, total.shape, 0) == 0
    publish(0, jnp.where(first_row, early_inv[1, pl.ds(me, 1), :], total))

    def first_spread(j):
        spread(0, j, late)
        if experts > 1:
            load(1, peer(j)).start()
        if rest:
            bulk_rest(j, peer(j), me).start()

    each(n - 1, first_spread)
    keep(0)
    if experts > 1:
        load(1, me).start()

    each(n - 1, lambda j: router_copy(peer(j), peer(j)).wait_recv())
    each(m - 1, lambda j: group_copy(mate(j), group).start())

    def expert(k):
        e = k + 1

        def some_sums(j):
            d = peer(j)
            load(e, d).wait()
            partial(e, d, spans)
            sums(e, d, me).start()

        each(n - 1, some_sums)
        load(e, me).wait()
        partial(e, me, spans)
        publish(e, add_up(e))

        @pl.when(e >= 2)
        def _():
            local(e - 2).wait()

        def some_spread(j):
            spread(e, j, spans)

            @pl.when(e + 1 < experts)
            def _():
                load(e + 1, peer(j)).start()

            bulk(e, j, peer(j), me).start()

        each(n - 1, some_spread)
        keep(e)

        @pl.when(e + 1 < experts)
        def _():
            load(e + 1, me).start()

    if experts > 1:
        each(experts - 1, expert)

    each(m - 1, lambda j: group_copy(mate(j), mate(j)).wait_recv())
    lines = rbuf.shape[1]
    for g in range(m):
        rwide[g * lines:(g + 1) * lines, :] = rbuf[g].astype(jnp.float32)
    router_v[...] = rwide[...].astype(jnp.bfloat16)
    for e in range(experts):
        sc_v[e:e + 1, :] = sc_rows[e]
    put_router = pltpu.make_async_copy(router_v, router, out_sem.at[0])
    put_scale = pltpu.make_async_copy(sc_v, sc, out_sem.at[1])
    put_router.start()
    put_scale.start()

    for e in range(max(0, experts - 2), experts):
        local(e).wait()

    def finish(j):
        d = peer(j)
        early_copy(d, me).wait_send()
        router_copy(d, me).wait_send()
        bulk_head(j, d, me).wait_send()
        bulk_head(j, d, d).wait_recv()
        if rest:
            bulk_rest(j, d, me).wait_send()
            bulk_rest(j, d, d).wait_recv()
        sums(0, d, me).wait_send()
        scale_copy(0, d, me).wait_send()

        def more(k):
            e = k + 1
            sums(e, d, me).wait_send()
            scale_copy(e, d, me).wait_send()
            bulk(e, j, d, me).wait_send()
            bulk(e, j, d, d).wait_recv()

        if experts > 1:
            each(experts - 1, more)

    each(n - 1, finish)
    each(m - 1, lambda j: group_copy(mate(j), group).wait_send())
    put_router.wait()
    put_scale.wait()


def exchange(n, m, w, rw, gain):
    experts, rows, cols = w.shape
    lines, width = rw.shape
    block = rows // n
    tiles = -(-block // LANES)
    padded = ceil_to(tiles, 8)
    depth = ceil_to(n, 8)
    dma = pltpu.SemaphoreType.DMA
    f32, bf16 = jnp.float32, jnp.bfloat16
    buffers = [
        ((n, block, cols), f32),
        ((experts, n - 1, block, cols), bf16),
        ((2, block, cols), bf16),
        ((n, depth, LANES), f32),
        ((2, depth, LANES), f32),
        ((experts, n, padded, LANES), f32),
        ((experts, n, padded, LANES), f32),
        ((experts, padded, LANES), f32),
        ((experts, n, padded, LANES), f32),
        ((lines, width), f32),
        ((1, width), f32),
        ((m, lines, n * width), bf16),
        ((m * lines, n * width), f32),
        ((m * lines, n * width), bf16),
        ((experts, block), f32),
        ((experts, 1, block), f32),
    ]
    size = sum(functools.reduce(lambda a, b: a * b, s) * jnp.dtype(t).itemsize for s, t in buffers)
    return pl.pallas_call(
        functools.partial(kernel, n, m),
        out_shape=(
            jax.ShapeDtypeStruct((experts, block, n * cols), bf16),
            jax.ShapeDtypeStruct((experts, block), f32),
            jax.ShapeDtypeStruct((m * lines, n * width), bf16),
        ),
        in_specs=[pl.BlockSpec(memory_space=pltpu.HBM)] * 3,
        out_specs=(pl.BlockSpec(memory_space=pl.ANY),) * 3,
        scratch_shapes=[pltpu.VMEM(s, t) for s, t in buffers] + [
            dma((n,)), dma((n,)), dma((2,)), dma((n,)), dma((n,)),
            dma((experts, n)), dma((experts, n)), dma((experts, n)), dma((experts, n)),
            dma((n,)), dma((n,)), dma((experts, n)), dma((experts, n)), dma((2,)),
            dma((n,)), dma((n,)), dma((m,)), dma((m,)), dma((2,)),
        ],
        compiler_params=pltpu.CompilerParams(
            collective_id=0, has_side_effects=True,
            vmem_limit_bytes=ceil_to(size + 6 * 512 * 1024, 512 * 1024)),
    )(w, rw, gain)


def body(n, m, w_down, router_weight, router_gain):
    serve_down, scale_down, router = exchange(n, m, w_down, router_weight.T, router_gain[None, :])
    return (serve_down, scale_down, router.T)


def solution(mesh):
    in_specs = (P("ep", None, "fsdp"), P("fsdp", "ep"), P("fsdp"))
    out_specs = (P("ep", "fsdp", None), P("ep", "fsdp"), P())
    return jax.shard_map(
        functools.partial(body, mesh.shape["fsdp"], mesh.shape["ep"]), mesh=mesh,
        in_specs=in_specs, out_specs=out_specs, check_vma=False)
```

time: 647 us -> 622 us (0.961)
  blocking collectives: 176 us -> 0 us
  Pallas kernels: 449 us -> 600 us
    all_gather x2 -> x0, blocking collectives: 176 us -> none  [the longest x1 171 us: body(): row_router = lax.all_gather(part_router, 'fsdp', axis=0, tiled=True)]
    pallas_call x1, Pallas kernels: 449 us -> 600 us  [exchange(): pl.pallas_call(functools.partial(kernel, n, m), out_shape=(jax.ShapeDtype...]
    unnamed x8 -> x7, local copies, waits for them, and re-layouts: 19.4 us -> 20.6 us
where the time goes in v1:
time: 622 us; the launch traced here: 621 us
  Pallas kernels  600 us (96%)
  local copies, waits for them, and re-layouts  20.6 us (3%)
    pallas_call x1, Pallas kernels, exchange(): pl.pallas_call(functools.partial(kernel, n, m), out_shape=(jax.ShapeDtype...  600 us
    unnamed x7, local copies, waits for them, and re-layouts  20.6 us

profile of v1, /device:TPU:0, one launch (start us, length us, event | category | flops | bytes accessed | tf_op | source)
XLA Modules:
  0.0 621.4 jit_solution(14109358884088371034)
XLA Ops:
  0.6 0.0 copy-start
  0.6 0.7 copy-done
  1.3 0.0 copy-start.1
  1.3 0.7 copy-done.1
  2.0 600.2 %shard_map.58 = (bf16[4,800,4096]{2,1,0:T(8,128)(2,1)}, f32[4,800]{1,0:T(4,128)S(1)}, bf16[16,4096]{1,0:T(8,128)(2,1)S(1)}) custom-call(f32[4,6400,512]{2,1,0:T(8,128)} %w.1, f32[4,512]{1,0:T(4,128)S(1)} %bitcast.4, f32[1,512]{1,0:T(1,128)S(1)} %bitcast.5), custom_call_target="tpu_custom_call" | custom-call | tf_op jit(solution)/shard_map/pallas_call | solution.py:357
  602.2 18.0 %copy.9 = bf16[4,800,4096]{2,1,0:T(8,128)(2,1)} copy(bf16[4,800,4096]{2,1,0:T(8,128)(2,1)} %get-tuple-element.12) | data formatting | bytes 52428800
  620.2 0.6 copy.10
  620.8 0.7 copy.11
Async XLA Ops:
  0.6 0.7 copy-start
  1.3 0.7 copy-start.1

commit v2 on v1

v2 whole, which is shorter than its diff:
```python
import functools

import jax
import jax.numpy as jnp
from jax import lax
from jax.experimental import pallas as pl
from jax.experimental.pallas import tpu as pltpu
from jax.sharding import PartitionSpec as P

LANES = 128
TAIL_START = 32
VMEM_BYTES = 67043328
MESH = pl.DeviceIdType.MESH


def each(count, f):
    def step(i, c):
        f(i)
        return c
    lax.fori_loop(0, count, step, 0)


def cuts(rows):
    first, second = ceil_to(rows * 48 // 128, 16), ceil_to(rows * 32 // 128, 16)
    return [(0, first), (first, second), (first + second, rows - first - second)]


def ceil_to(a, b):
    return -(-a // b) * b


def kernel(n, m, w, rw, gain, o, sc, router, tail,
           xbuf, sbuf, own, early, totals, part, recvp, mine, scales,
           rw_v, gain_v, rbuf, rwide, router_v, sc_v, sc_rows,
           head_sem, load_sem, arg_sem, esend, erecv, psend, precv, ssend, srecv,
           hsend, hrecv, bsend, brecv, own_sem, rsend, rrecv, gsend, grecv, out_sem):
    experts, rows, cols = w.shape
    block = rows // n
    tiles = -(-block // LANES)
    padded = part.shape[2]
    spans = [(t, t * LANES, min(LANES, block - t * LANES)) for t in range(tiles)]
    leads = early.shape[0]
    begin = min(leads * LANES, block)
    rest = block - begin
    late = spans[leads:]
    width = rw.shape[1]
    last = experts - 2 if experts > 2 else 1
    far = n // 2 - 1
    keep_back = tail.shape[0]
    short = block - keep_back
    me = lax.axis_index("fsdp")
    group = lax.axis_index("ep")

    pieces = cuts(min(LANES, block))

    def peer(j):
        return (me + 1 + j) % n

    def mate(j):
        return (group + 1 + j) % m

    def block_of(source):
        return pl.ds(pl.multiple_of(source * cols, LANES), cols)

    def send(src, dst, s, r, **to):
        return pltpu.make_async_remote_copy(
            src_ref=src, dst_ref=dst, send_sem=s, recv_sem=r,
            device_id=to, device_id_type=MESH)

    def load_part(d, start, count, sem):
        return pltpu.make_async_copy(
            w.at[0, pl.ds(pl.multiple_of(d * block + start, 8), count), :],
            xbuf.at[0, d, pl.ds(start, count), :], sem)

    def load_lead(t, d):
        return load_part(d, spans[t][1], spans[t][2], head_sem.at[t, d])

    def load_rest(d):
        return load_part(d, begin, rest, load_sem.at[0, d])

    def load(e, g, d):
        return pltpu.make_async_copy(
            w.at[e, pl.ds(pl.multiple_of(d * block, 8), block), :],
            xbuf.at[g, d], load_sem.at[g, d])

    def early_copy(t, to, source):
        return send(early.at[t, me], early.at[t, source],
                    esend.at[t, to], erecv.at[t, source], fsdp=to)

    def sums(e, to, source):
        return send(part.at[e, to], recvp.at[e, source],
                    psend.at[e, to], precv.at[e, source], fsdp=to)

    def scale_copy(e, to, source):
        return send(mine.at[e], scales.at[e, source],
                    ssend.at[e, to], srecv.at[e, source], fsdp=to)

    def piece_copy(p, j, to, source):
        start, count = pieces[p]
        return send(sbuf.at[0, j, pl.ds(start, count), :],
                    o.at[0, pl.ds(start, count), block_of(source)],
                    hsend.at[p, j], hrecv.at[p, source], fsdp=to)

    def bulk_rest(j, to, source):
        return send(sbuf.at[0, j, pl.ds(begin, rest), :],
                    o.at[0, pl.ds(begin, rest), block_of(source)],
                    bsend.at[0, j], brecv.at[0, source], fsdp=to)

    def bulk(e, j, to, source):
        return send(sbuf.at[e, j], o.at[e, :, block_of(source)],
                    bsend.at[e, j], brecv.at[e, source], fsdp=to)

    def bulk_short(to, source):
        return send(sbuf.at[last, far, pl.ds(0, short), :],
                    o.at[last, pl.ds(0, short), block_of(source)],
                    bsend.at[last, far], brecv.at[last, source], fsdp=to)

    def to_tail():
        return pltpu.make_async_copy(
            sbuf.at[last, far, pl.ds(short, keep_back), :], tail, out_sem.at[2])

    def local(e, s):
        return pltpu.make_async_copy(own.at[s], o.at[e, :, block_of(me)], own_sem.at[s])

    def router_copy(to, source):
        where = pl.ds(pl.multiple_of(source * width, LANES), width)
        return send(rbuf.at[group, :, where], rbuf.at[group, :, where],
                    rsend.at[to], rrecv.at[source], fsdp=to)

    def group_copy(to, source):
        return send(rbuf.at[source], rbuf.at[source], gsend.at[to], grecv.at[source], ep=to)

    def row_sums(g, d, start, count):
        x = xbuf[g, d, start:start + count, :]
        y = x * x
        acc = y[:, :LANES]
        for c in range(LANES, cols, LANES):
            acc = acc + y[:, c:c + LANES]
        if count < LANES:
            acc = jnp.concatenate([acc, jnp.zeros((LANES - count, LANES), jnp.float32)], axis=0)
        return jnp.sum(acc.T, axis=0, keepdims=True)

    def scaled(g, d, inverse, t, start, count, store):
        first = start - t * LANES
        factor = jnp.broadcast_to(inverse, (LANES, LANES)).T[first:first + count]
        for c in range(0, cols, LANES):
            x = xbuf[g, d, start:start + count, c:c + LANES]
            store(start, count, c, (x * factor).astype(jnp.bfloat16))

    def into(e, j):
        def store(start, count, c, value):
            sbuf[e, j, start:start + count, c:c + LANES] = value
        return store

    get_rw = pltpu.make_async_copy(rw, rw_v, arg_sem.at[0])
    get_gain = pltpu.make_async_copy(gain, gain_v, arg_sem.at[1])

    barrier = pltpu.get_barrier_semaphore()
    each(n - 1, lambda j: pl.semaphore_signal(
        barrier, inc=1, device_id={"fsdp": peer(j)}, device_id_type=MESH))
    each(m - 1, lambda j: pl.semaphore_signal(
        barrier, inc=1, device_id={"ep": mate(j)}, device_id_type=MESH))
    for t in range(leads):
        each(n, lambda d: load_lead(t, d).start())
    get_rw.start()
    get_gain.start()
    if rest:
        each(n, lambda d: load_rest(d).start())
    if experts > 1:
        each(n, lambda d: load(1, 1, d).start())

    for t in range(leads):
        def lead_sums(d):
            load_lead(t, d).wait()
            early[t, me, pl.ds(d, 1), :] = row_sums(0, d, *spans[t][1:])

        each(n, lead_sums)
        if t == 0:
            pl.semaphore_wait(barrier, n - 1 + m - 1)
        each(n - 1, lambda j: early_copy(t, peer(j), me).start())

    get_rw.wait()
    get_gain.wait()
    rbuf[group, :, pl.ds(pl.multiple_of(me * width, LANES), width)] = (
        rw_v[...] * gain_v[...]).astype(jnp.bfloat16)

    def lead_totals(t):
        each(n - 1, lambda j: early_copy(t, peer(j), peer(j)).wait_recv())
        total = early[t, 0]
        for s in range(1, n):
            total = total + early[t, s]
        totals[t, 0] = total
        totals[t, 1] = 1.0 / jnp.sqrt(total)

    def send_piece(p):
        start, count = pieces[p]
        t = start // LANES

        def one(j):
            d = peer(j)
            scaled(0, d, totals[t, 1, pl.ds(d, 1), :], t, start, count, into(0, j))
            piece_copy(p, j, d, me).start()

        each(n - 1, one)

    lead_totals(0)
    send_piece(0)
    each(n - 1, lambda j: router_copy(peer(j), me).start())

    def partial(e, g, d, which):
        found = [jnp.zeros((1, LANES), jnp.float32)] * (tiles - len(which))
        found += [row_sums(g, d, start, count) for _, start, count in which]
        if padded > tiles:
            found.append(jnp.zeros((padded - tiles, LANES), jnp.float32))
        part[e, d] = jnp.concatenate(found, axis=0)

    def first_sums(j):
        d = peer(j)
        if rest:
            load_rest(d).wait()
            partial(0, 0, d, late)
            sums(0, d, me).start()

    each(n - 1, first_sums)
    if rest:
        load_rest(me).wait()
    partial(0, 0, me, late)

    def more_sums(k):
        e = k + 1

        def one(j):
            d = peer(j)
            load(e, 1, d).wait()
            partial(e, 1, d, spans)

            @pl.when(e + 1 < experts)
            def _():
                load(e + 1, 1, d).start()

            @pl.when(j < n - 1)
            def _():
                sums(e, d, me).start()

        each(n, one)

    if experts > 1:
        each(experts - 1, more_sums)

    for t in range(1, leads):
        lead_totals(t)
    if len(pieces) > 1:
        send_piece(1)

    def publish(e, total):
        scale = jnp.sqrt(total)
        inverse = 1.0 / scale
        mine[e] = inverse
        scales[e, me] = inverse
        for t, start, count in spans:
            sc_rows[e, :, start:start + count] = scale[t:t + 1, :count]

    def add_up(e):
        def add(j, total):
            source = peer(j)
            sums(e, source, source).wait_recv()
            return total + recvp[e, source]

        return lax.fori_loop(0, n - 1, add, part[e, me])

    total = add_up(0) if rest else part[0, me]
    row = lax.broadcasted_iota(jnp.int32, total.shape, 0)
    for t in range(leads):
        total = jnp.where(row == t, totals[t, 0, pl.ds(me, 1), :], total)
    publish(0, total)
    if rest:
        each(n - 1, lambda j: scale_copy(0, peer(j), me).start())

    def more_scales(k):
        publish(k + 1, add_up(k + 1))
        each(n - 1, lambda j: scale_copy(k + 1, peer(j), me).start())

    if experts > 1:
        each(experts - 1, more_scales)

    for p in range(2, len(pieces)):
        send_piece(p)

    def keep(e, g, s):
        def store(start, count, c, value):
            own[s, start:start + count, c:c + LANES] = value

        inverse = scales[e, me]
        for t, start, count in spans:
            scaled(g, me, inverse[t:t + 1, :], t, start, count, store)
        local(e, s).start()

    def expert_at(k):
        return (k + experts - 3) % (experts - 1) + 1

    def refill(k, d):
        if experts > 3:
            @pl.when(k + 2 < experts)
            def _():
                load(expert_at(k + 2), k % 2, d).start()

    def first_rest(j):
        d = peer(j)
        if rest:
            scale_copy(0, d, d).wait_recv()
            inverse = scales[0, d]
            for t, start, count in late:
                scaled(0, d, inverse[t:t + 1, :], t, start, count, into(0, j))
            bulk_rest(j, d, me).start()
        if experts > 2:
            load(expert_at(2), 0, d).start()

    each(n - 1, first_rest)
    keep(0, 0, 0)
    if experts > 2:
        load(expert_at(2), 0, me).start()

    each(n - 1, lambda j: router_copy(peer(j), peer(j)).wait_recv())
    each(m - 1, lambda j: group_copy(mate(j), group).start())

    def more(i):
        k = i + 1
        e = expert_at(k)
        g = k % 2

        def one(j):
            d = peer(j)
            scale_copy(e, d, d).wait_recv()

            @pl.when(k >= 2)
            def _():
                load(e, g, d).wait()

            inverse = scales[e, d]
            for t, start, count in spans:
                scaled(g, d, inverse[t:t + 1, :], t, start, count, into(e, j))
            refill(k, d)
            cut = (e == last) & (j == far)

            @pl.when(cut)
            def _():
                bulk_short(d, me).start()
                to_tail().start()

            @pl.when(jnp.logical_not(cut))
            def _():
                bulk(e, j, d, me).start()

        each(n - 1, one)

        @pl.when(k >= 2)
        def _():
            load(e, g, me).wait()
            local(e, g).wait()

        keep(e, g, g)
        refill(k, me)

    if experts > 1:
        each(experts - 1, more)

    each(m - 1, lambda j: group_copy(mate(j), mate(j)).wait_recv())
    lines = rbuf.shape[1]
    for g in range(m):
        rwide[g * lines:(g + 1) * lines, :] = rbuf[g].astype(jnp.float32)
    router_v[...] = rwide[...].astype(jnp.bfloat16)
    for e in range(experts):
        sc_v[e:e + 1, :] = sc_rows[e]
    put_router = pltpu.make_async_copy(router_v, router, out_sem.at[0])
    put_scale = pltpu.make_async_copy(sc_v, sc, out_sem.at[1])
    put_router.start()
    put_scale.start()

    for s in range(min(experts, 2)):
        local(0, s).wait()

    def finish(j):
        d = peer(j)
        for t in range(leads):
            early_copy(t, d, me).wait_send()
        router_copy(d, me).wait_send()
        for p in range(len(pieces)):
            piece_copy(p, j, d, me).wait_send()
            piece_copy(p, j, d, d).wait_recv()
        if rest:
            sums(0, d, me).wait_send()
            scale_copy(0, d, me).wait_send()
            bulk_rest(j, d, me).wait_send()
            bulk_rest(j, d, d).wait_recv()

        def other(k):
            e = k + 1
            sums(e, d, me).wait_send()
            scale_copy(e, d, me).wait_send()
            cut = (e == last) & (j == far)

            @pl.when(cut)
            def _():
                bulk_short(d, me).wait_send()
                bulk_short(d, d).wait_recv()

            @pl.when(jnp.logical_not(cut))
            def _():
                bulk(e, j, d, me).wait_send()
                bulk(e, j, d, d).wait_recv()

        if experts > 1:
            each(experts - 1, other)

    each(n - 1, finish)
    each(m - 1, lambda j: group_copy(mate(j), group).wait_send())
    put_router.wait()
    put_scale.wait()
    to_tail().wait()


def exchange(n, m, w, rw, gain):
    experts, rows, cols = w.shape
    lines, width = rw.shape
    block = rows // n
    tiles = -(-block // LANES)
    padded = ceil_to(tiles, 8)
    depth = ceil_to(n, 8)
    leads = 1
    keep_back = tail_rows(block)
    pieces = len(cuts(min(LANES, block)))
    dma = pltpu.SemaphoreType.DMA
    f32, bf16 = jnp.float32, jnp.bfloat16
    buffers = [
        ((2, n, block, cols), f32),
        ((experts, n - 1, block, cols), bf16),
        ((2, block, cols), bf16),
        ((leads, n, depth, LANES), f32),
        ((leads, 2, depth, LANES), f32),
        ((experts, n, padded, LANES), f32),
        ((experts, n, padded, LANES), f32),
        ((experts, padded, LANES), f32),
        ((experts, n, padded, LANES), f32),
        ((lines, width), f32),
        ((1, width), f32),
        ((m, lines, n * width), bf16),
        ((m * lines, n * width), f32),
        ((m * lines, n * width), bf16),
        ((experts, block), f32),
        ((experts, 1, block), f32),
    ]
    return pl.pallas_call(
        functools.partial(kernel, n, m),
        out_shape=(
            jax.ShapeDtypeStruct((experts, block, n * cols), bf16),
            jax.ShapeDtypeStruct((experts, block), f32),
            jax.ShapeDtypeStruct((m * lines, n * width), bf16),
            jax.ShapeDtypeStruct((keep_back, cols), bf16),
        ),
        in_specs=[pl.BlockSpec(memory_space=pltpu.HBM)] * 3,
        out_specs=(pl.BlockSpec(memory_space=pl.ANY),) * 4,
        scratch_shapes=[pltpu.VMEM(s, t) for s, t in buffers] + [
            dma((leads, n)), dma((2, n)), dma((2,)), dma((leads, n)), dma((leads, n)),
            dma((experts, n)), dma((experts, n)), dma((experts, n)), dma((experts, n)),
            dma((pieces, n)), dma((pieces, n)), dma((experts, n)), dma((experts, n)), dma((2,)),
            dma((n,)), dma((n,)), dma((m,)), dma((m,)), dma((3,)),
        ],
        compiler_params=pltpu.CompilerParams(
            collective_id=0, has_side_effects=True,
            vmem_limit_bytes=VMEM_BYTES),
    )(w, rw, gain)


def tail_rows(block):
    start = ceil_to(block * TAIL_START // 100, 16)
    return block - start


def settle_kernel(o, sc, router, full, sc_out, router_out, buf, sc_v, router_v, get, put):
    experts, block, _ = o.shape
    parts = get.shape[0] - 1
    rows = block * experts // (parts - 1)
    per = block // rows
    pairs = [(sc, sc_v, sc_out), (router, router_v, router_out)]

    def where(i):
        return i // per, pl.ds(pl.multiple_of(i % per * rows, 8), rows)

    def load(i):
        e, r = where(i)
        return pltpu.make_async_copy(o.at[e, r, :], buf.at[e, r, :], get.at[i])

    def save(i):
        e, r = where(i)
        return pltpu.make_async_copy(buf.at[e, r, :], full.at[e, r, :], put.at[i])

    def load_small(i):
        return pltpu.make_async_copy(pairs[i][0], pairs[i][1], get.at[parts - 1 + i])

    def save_small(i):
        return pltpu.make_async_copy(pairs[i][1], pairs[i][2], put.at[parts - 1 + i])

    each(parts - 1, lambda i: load(i).start())
    for i in range(2):
        load_small(i).start()

    def move(i):
        load(i).wait()
        save(i).start()

    each(parts - 1, move)
    for i in range(2):
        load_small(i).wait()
        save_small(i).start()
    each(parts - 1, lambda i: save(i).wait())
    for i in range(2):
        save_small(i).wait()


def settle(o, sc, router):
    experts, block, _ = o.shape
    per = max(p for p in (1, 2, 4, 5) if p == 1 or block % (16 * p) == 0)
    count = experts * per + 2
    dma = pltpu.SemaphoreType.DMA
    return pl.pallas_call(
        settle_kernel,
        out_shape=tuple(jax.ShapeDtypeStruct(a.shape, a.dtype) for a in (o, sc, router)),
        in_specs=[pl.BlockSpec(memory_space=pltpu.HBM)] * 3,
        out_specs=(pl.BlockSpec(memory_space=pltpu.HBM),) * 3,
        scratch_shapes=[pltpu.VMEM(a.shape, a.dtype) for a in (o, sc, router)] + [
            dma((count,)), dma((count,))],
        cost_estimate=pl.CostEstimate(flops=0, bytes_accessed=4 * o.size, transcendentals=0),
        compiler_params=pltpu.CompilerParams(vmem_limit_bytes=48 * 1024 * 1024),
    )(o, sc, router)


def place_kernel(n, expert, full, got, out, sem):
    del full
    rows, cols = got.shape
    source = (lax.axis_index("fsdp") + n // 2) % n
    copy = pltpu.make_async_copy(
        got, out.at[expert, pl.ds(out.shape[1] - rows, rows),
                    pl.ds(pl.multiple_of(source * cols, LANES), cols)], sem)
    copy.start()
    copy.wait()


def place(n, expert, full, got):
    return pl.pallas_call(
        functools.partial(place_kernel, n, expert),
        out_shape=jax.ShapeDtypeStruct(full.shape, full.dtype),
        in_specs=[pl.BlockSpec(memory_space=pltpu.HBM), pl.BlockSpec(memory_space=pltpu.VMEM)],
        out_specs=pl.BlockSpec(memory_space=pltpu.HBM),
        scratch_shapes=[pltpu.SemaphoreType.DMA],
        input_output_aliases={0: 0},
        compiler_params=pltpu.CompilerParams(vmem_limit_bytes=8 * 1024 * 1024),
    )(full, got)


def body(n, m, w_down, router_weight, router_gain):
    experts = w_down.shape[0]
    o, scale, router, tail = exchange(n, m, w_down, router_weight.T, router_gain[None, :])
    got = lax.ppermute(tail, "fsdp", [(i, (i + n // 2) % n) for i in range(n)])
    full, scale, router = settle(o, scale, router)
    serve_down = place(n, experts - 2 if experts > 2 else 1, full, got)
    return (serve_down, scale, router.T)


def solution(mesh):
    in_specs = (P("ep", None, "fsdp"), P("fsdp", "ep"), P("fsdp"))
    out_specs = (P("ep", "fsdp", None), P("ep", "fsdp"), P())
    return jax.shard_map(
        functools.partial(body, mesh.shape["fsdp"], mesh.shape["ep"]), mesh=mesh,
        in_specs=in_specs, out_specs=out_specs, check_vma=False)
```

time: 622 us -> 583 us (0.937)
  Pallas kernels: 600 us -> 537 us
  starting transfers between devices: 0 us -> 39.1 us
  local copies, waits for them, and re-layouts: 20.6 us -> 1.62 us
    pallas_call x1, Pallas kernels: 600 us -> 518 us  [exchange(): pl.pallas_call(functools.partial(kernel, n, m), out_shape=(jax.ShapeDtype...]
    ppermute x0 -> x1, starting transfers between devices: none -> 39.1 us  [body(): got = lax.ppermute(tail, 'fsdp', [(i, (i + n // 2) % n) for i in range(n)])]
    unnamed x7 -> x4, local copies, waits for them, and re-layouts: 20.6 us -> 1.62 us
    pallas_call x0 -> x2, Pallas kernels: none -> 18.9 us  [the longest x1 18.1 us: settle(): pl.pallas_call(settle_kernel, out_shape=tuple((jax.ShapeDtypeStruct(a.sha...]
  transfers between devices with their start and end apart: 0 -> 1, of which waited for: 0 -> 1; matrix products, arithmetic and copies ran while one was open for 0% -> 0% of each run, Pallas kernels for 0% -> 3%
where the time goes in v2:
time: 583 us
  Pallas kernels  537 us (92%)
  starting transfers between devices  39.1 us (7%)
    pallas_call x1, Pallas kernels, exchange(): pl.pallas_call(functools.partial(kernel, n, m), out_shape=(jax.ShapeDtype...  518 us
    ppermute x1, starting transfers between devices, body(): got = lax.ppermute(tail, 'fsdp', [(i, (i + n // 2) % n) for i in range(n)])  39.1 us
    pallas_call x1, Pallas kernels, settle(): pl.pallas_call(settle_kernel, out_shape=tuple((jax.ShapeDtypeStruct(a.sha...  18.1 us
  transfers between devices with their start and end apart: 1, of which 1 were waited for; matrix products, arithmetic and copies ran while one was open for 0% of the time, Pallas kernels for 3%

profile of v2, /device:TPU:0, one launch (start us, length us, event | category | flops | bytes accessed | tf_op | source)
XLA Modules:
  0.0 582.6 jit_solution(14002969787773213284)
XLA Ops:
  0.6 518.3 %shard_map.58 = (bf16[4,800,4096]{2,1,0:T(8,128)(2,1)}, f32[4,800]{1,0:T(4,128)}, bf16[16,4096]{1,0:T(8,128)(2,1)}, bf16[544,512]{1,0:T(8,128)(2,1)}) custom-call(f32[4,6400,512]{2,1,0:T(8,128)} %w.1, f32[4,512]{1,0:T(4,128)} %bitcast.3, f32[1,512]{1,0:T(1,128)} %bitcast.4), custom_call_target="tpu_custom_call" | custom-call | tf_op jit(solution)/shard_map/pallas_call | solution.py:452
  518.9 39.1 %collective-permute-start = (bf16[544,512]{1,0:T(8,128)(2,1)}, bf16[544,512]{1,0:T(8,128)(2,1)S(1)}, u32[]{:S(2)}, u32[]{:S(2)}) collective-permute-start(bf16[544,512]{1,0:T(8,128)(2,1)} %get-tuple-element.14), channel_id=1, source_target_pairs={{0,4},{1,5},{2,6},{3,7},{4,0},{5,1},{6,2},{7,3},{8,12},{9,13},{10,... | collective-permute-start | bytes 1671176 | tf_op jit(solution)/shard_map/ppermute | solution.py:563
  558.0 0.0 copy-start
  558.0 0.9 copy-done
  558.9 0.0 copy-start.1
  558.9 0.7 copy-done.1
  559.6 18.1 %shard_map.59 = (bf16[4,800,4096]{2,1,0:T(8,128)(2,1)}, f32[4,800]{1,0:T(4,128)}, bf16[16,4096]{1,0:T(8,128)(2,1)}) custom-call(bf16[4,800,4096]{2,1,0:T(8,128)(2,1)} %get-tuple-element.10.o, f32[4,800]{1,0:T(4,128)S(1)} %copy-done.1, bf16[16,4096]{1,0:T(8,128)(2,1)S(1)} %copy-done), custom_call_target="tpu_custom_call" | custom-call | bytes 52428800 | tf_op jit(solution)/shard_map/pallas_call | solution.py:525
  577.7 4.1 collective-permute-done.got
  581.8 0.8 shard_map.60
Async XLA Ops:
  518.9 62.9 %collective-permute-start = (bf16[544,512]{1,0:T(8,128)(2,1)}, bf16[544,512]{1,0:T(8,128)(2,1)S(1)}, u32[]{:S(2)}, u32[]{:S(2)}) collective-permute-start(bf16[544,512]{1,0:T(8,128)(2,1)} %get-tuple-element.14), channel_id=1, source_target_pairs={{0,4},{1,5},{2,6},{3,7},{4,0},{5,1},{6,2},{7,3},{8,12},{9,13},{10,... | collective-permute-start | bytes 1671176 | tf_op jit(solution)/shard_map/ppermute | solution.py:563
  558.0 0.9 copy-start
  558.9 0.7 copy-start.1

commit v3 on v2

--- a/solution.py
+++ b/solution.py
@@ -9,6 +9,8 @@
 
 LANES = 128
 TAIL_START = 32
+LEADS = 2
+CUTS = (64, 96, 128, 160)
 VMEM_BYTES = 67043328
 MESH = pl.DeviceIdType.MESH
 
@@ -21,8 +23,9 @@
 
 
 def cuts(rows):
-    first, second = ceil_to(rows * 48 // 128, 16), ceil_to(rows * 32 // 128, 16)
-    return [(0, first), (first, second), (first + second, rows - first - second)]
+    ends = [c for c in CUTS if c < rows] + [rows]
+    starts = [0] + ends[:-1]
+    return [(a, b - a) for a, b in zip(starts, ends)]
 
 
 def ceil_to(a, b):
@@ -30,9 +33,9 @@
 
 
 def kernel(n, m, w, rw, gain, o, sc, router, tail,
-           xbuf, sbuf, own, early, totals, part, recvp, mine, scales,
+           xbuf, sbuf, own, early, totals, part, recvp, pair, scales,
            rw_v, gain_v, rbuf, rwide, router_v, sc_v, sc_rows,
-           head_sem, load_sem, arg_sem, esend, erecv, psend, precv, ssend, srecv,
+           head_sem, load_sem, arg_sem, esend, erecv, psend, precv, msend, mrecv, csend, crecv,
            hsend, hrecv, bsend, brecv, own_sem, rsend, rrecv, gsend, grecv, out_sem):
     experts, rows, cols = w.shape
     block = rows // n
@@ -50,11 +53,19 @@
     short = block - keep_back
     me = lax.axis_index("fsdp")
     group = lax.axis_index("ep")
-
-    pieces = cuts(min(LANES, block))
+    half = n // 2
+    side, rank = me // half, me % half
+
+    pieces = cuts(begin)
 
     def peer(j):
         return (me + 1 + j) % n
+
+    def order(q):
+        return (me + (1 + q)) % n
+
+    def place_in(d):
+        return (me * (n - 1) + d + n - 1) % n
 
     def mate(j):
         return (group + 1 + j) % m
@@ -87,13 +98,23 @@
         return send(early.at[t, me], early.at[t, source],
                     esend.at[t, to], erecv.at[t, source], fsdp=to)
 
-    def sums(e, to, source):
-        return send(part.at[e, to], recvp.at[e, source],
-                    psend.at[e, to], precv.at[e, source], fsdp=to)
-
-    def scale_copy(e, to, source):
-        return send(mine.at[e], scales.at[e, source],
-                    ssend.at[e, to], srecv.at[e, source], fsdp=to)
+    def neighbour(g):
+        return side * half + g
+
+    def sums(e, d, source):
+        return send(part.at[e, d], recvp.at[e, source, d // half],
+                    psend.at[e, d], precv.at[e, source * 2 + d // half],
+                    fsdp=neighbour(d % half))
+
+    def across(source):
+        return send(pair.at[source], pair.at[source], msend, mrecv, fsdp=(me + half) % n)
+
+    def scale_copy(to, source):
+        return send(scales.at[source], scales.at[source],
+                    csend.at[to], crecv.at[source], fsdp=neighbour(to))
+
+    def other(j):
+        return (rank + 1 + j) % half
 
     def piece_copy(p, j, to, source):
         start, count = pieces[p]
@@ -183,6 +204,7 @@
     get_gain.wait()
     rbuf[group, :, pl.ds(pl.multiple_of(me * width, LANES), width)] = (
         rw_v[...] * gain_v[...]).astype(jnp.bfloat16)
+    each(n - 1, lambda j: router_copy(peer(j), me).start())
 
     def lead_totals(t):
         each(n - 1, lambda j: early_copy(t, peer(j), peer(j)).wait_recv())
@@ -196,8 +218,9 @@
         start, count = pieces[p]
         t = start // LANES
 
-        def one(j):
-            d = peer(j)
+        def one(q):
+            d = order(q)
+            j = place_in(d)
             scaled(0, d, totals[t, 1, pl.ds(d, 1), :], t, start, count, into(0, j))
             piece_copy(p, j, d, me).start()
 
@@ -205,7 +228,6 @@
 
     lead_totals(0)
     send_piece(0)
-    each(n - 1, lambda j: router_copy(peer(j), me).start())
 
     def partial(e, g, d, which):
         found = [jnp.zeros((1, LANES), jnp.float32)] * (tiles - len(which))
@@ -216,15 +238,15 @@
 
     def first_sums(j):
         d = peer(j)
-        if rest:
-            load_rest(d).wait()
-            partial(0, 0, d, late)
-            sums(0, d, me).start()
-
-    each(n - 1, first_sums)
+        load_rest(d).wait()
+        partial(0, 0, d, late)
+
+        @pl.when(d % half != rank)
+        def _():
+            sums(0, d, rank).start()
+
     if rest:
-        load_rest(me).wait()
-    partial(0, 0, me, late)
+        each(n, first_sums)
 
     def more_sums(k):
         e = k + 1
@@ -238,9 +260,9 @@
             def _():
                 load(e + 1, 1, d).start()
 
-            @pl.when(j < n - 1)
-            def _():
-                sums(e, d, me).start()
+            @pl.when(d % half != rank)
+            def _():
+                sums(e, d, rank).start()
 
         each(n, one)
 
@@ -252,45 +274,52 @@
     if len(pieces) > 1:
         send_piece(1)
 
-    def publish(e, total):
+    first_sum = 0 if rest else 1
+
+    def add_up(i):
+        e, b = first_sum + i // 2, i % 2
+
+        def add(j, total):
+            source = other(j)
+            sums(e, b * half + rank, source).wait_recv()
+            return total + recvp[e, source, b]
+
+        pair[side, e, b] = lax.fori_loop(0, half - 1, add, part[e, b * half + rank])
+
+    each(2 * (experts - first_sum), add_up)
+    across(side).start()
+
+    if len(pieces) > 2:
+        send_piece(2)
+
+    across(1 - side).wait_recv()
+
+    def scale_of(i):
+        e, b = i // 2, i % 2
+        total = pair[0, e, b] + pair[1, e, b]
+        row = lax.broadcasted_iota(jnp.int32, total.shape, 0)
+        for t in range(leads):
+            lead = totals[t, 0, pl.ds(b * half + rank, 1), :]
+            total = jnp.where((row == t) & (e == 0), lead, total)
         scale = jnp.sqrt(total)
-        inverse = 1.0 / scale
-        mine[e] = inverse
-        scales[e, me] = inverse
-        for t, start, count in spans:
-            sc_rows[e, :, start:start + count] = scale[t:t + 1, :count]
-
-    def add_up(e):
-        def add(j, total):
-            source = peer(j)
-            sums(e, source, source).wait_recv()
-            return total + recvp[e, source]
-
-        return lax.fori_loop(0, n - 1, add, part[e, me])
-
-    total = add_up(0) if rest else part[0, me]
-    row = lax.broadcasted_iota(jnp.int32, total.shape, 0)
-    for t in range(leads):
-        total = jnp.where(row == t, totals[t, 0, pl.ds(me, 1), :], total)
-    publish(0, total)
-    if rest:
-        each(n - 1, lambda j: scale_copy(0, peer(j), me).start())
-
-    def more_scales(k):
-        publish(k + 1, add_up(k + 1))
-        each(n - 1, lambda j: scale_copy(k + 1, peer(j), me).start())
-
-    if experts > 1:
-        each(experts - 1, more_scales)
-
-    for p in range(2, len(pieces)):
+        scales[rank, e, b] = 1.0 / scale
+
+        @pl.when(b == side)
+        def _():
+            for t, start, count in spans:
+                sc_rows[e, :, start:start + count] = scale[t:t + 1, :count]
+
+    each(2 * experts, scale_of)
+    each(half - 1, lambda j: scale_copy(other(j), rank).start())
+
+    for p in range(3, len(pieces)):
         send_piece(p)
 
     def keep(e, g, s):
         def store(start, count, c, value):
             own[s, start:start + count, c:c + LANES] = value
 
-        inverse = scales[e, me]
+        inverse = scales[rank, e, side]
         for t, start, count in spans:
             scaled(g, me, inverse[t:t + 1, :], t, start, count, store)
         local(e, s).start()
@@ -304,17 +333,18 @@
             def _():
                 load(expert_at(k + 2), k % 2, d).start()
 
-    def first_rest(j):
-        d = peer(j)
+    def first_rest(q):
+        d = order(q)
+        j = place_in(d)
         if rest:
-            scale_copy(0, d, d).wait_recv()
-            inverse = scales[0, d]
+            inverse = scales[d % half, 0, d // half]
             for t, start, count in late:
                 scaled(0, d, inverse[t:t + 1, :], t, start, count, into(0, j))
             bulk_rest(j, d, me).start()
         if experts > 2:
             load(expert_at(2), 0, d).start()
 
+    each(half - 1, lambda j: scale_copy(other(j), other(j)).wait_recv())
     each(n - 1, first_rest)
     keep(0, 0, 0)
     if experts > 2:
@@ -328,15 +358,15 @@
         e = expert_at(k)
         g = k % 2
 
-        def one(j):
-            d = peer(j)
-            scale_copy(e, d, d).wait_recv()
+        def one(q):
+            d = order(q)
+            j = place_in(d)
 
             @pl.when(k >= 2)
             def _():
                 load(e, g, d).wait()
 
-            inverse = scales[e, d]
+            inverse = scales[d % half, e, d // half]
             for t, start, count in spans:
                 scaled(g, d, inverse[t:t + 1, :], t, start, count, into(e, j))
             refill(k, d)
@@ -388,15 +418,20 @@
             piece_copy(p, j, d, me).wait_send()
             piece_copy(p, j, d, d).wait_recv()
         if rest:
-            sums(0, d, me).wait_send()
-            scale_copy(0, d, me).wait_send()
+            @pl.when(d % half != rank)
+            def _():
+                sums(0, d, rank).wait_send()
+
             bulk_rest(j, d, me).wait_send()
             bulk_rest(j, d, d).wait_recv()
 
-        def other(k):
+        def others(k):
             e = k + 1
-            sums(e, d, me).wait_send()
-            scale_copy(e, d, me).wait_send()
+
+            @pl.when(d % half != rank)
+            def _():
+                sums(e, d, rank).wait_send()
+
             cut = (e == last) & (j == far)
 
             @pl.when(cut)
@@ -410,9 +445,11 @@
                 bulk(e, j, d, d).wait_recv()
 
         if experts > 1:
-            each(experts - 1, other)
+            each(experts - 1, others)
 
     each(n - 1, finish)
+    each(half - 1, lambda j: scale_copy(other(j), rank).wait_send())
+    across(side).wait_send()
     each(m - 1, lambda j: group_copy(mate(j), group).wait_send())
     put_router.wait()
     put_scale.wait()
@@ -426,9 +463,9 @@
     tiles = -(-block // LANES)
     padded = ceil_to(tiles, 8)
     depth = ceil_to(n, 8)
-    leads = 1
+    leads = min(LEADS, tiles)
     keep_back = tail_rows(block)
-    pieces = len(cuts(min(LANES, block)))
+    pieces = len(cuts(min(leads * LANES, block)))
     dma = pltpu.SemaphoreType.DMA
     f32, bf16 = jnp.float32, jnp.bfloat16
     buffers = [
@@ -438,9 +475,9 @@
         ((leads, n, depth, LANES), f32),
         ((leads, 2, depth, LANES), f32),
         ((experts, n, padded, LANES), f32),
-        ((experts, n, padded, LANES), f32),
-        ((experts, padded, LANES), f32),
-        ((experts, n, padded, LANES), f32),
+        ((experts, n // 2, 2, padded, LANES), f32),
+        ((2, experts, 2, padded, LANES), f32),
+        ((n // 2, experts, 2, padded, LANES), f32),
         ((lines, width), f32),
         ((1, width), f32),
         ((m, lines, n * width), bf16),
@@ -461,7 +498,7 @@
         out_specs=(pl.BlockSpec(memory_space=pl.ANY),) * 4,
         scratch_shapes=[pltpu.VMEM(s, t) for s, t in buffers] + [
             dma((leads, n)), dma((2, n)), dma((2,)), dma((leads, n)), dma((leads, n)),
-            dma((experts, n)), dma((experts, n)), dma((experts, n)), dma((experts, n)),
+            dma((experts, n)), dma((experts, n)), dma, dma, dma((n,)), dma((n,)),
             dma((pieces, n)), dma((pieces, n)), dma((experts, n)), dma((experts, n)), dma((2,)),
             dma((n,)), dma((n,)), dma((m,)), dma((m,)), dma((3,)),
         ],

time: 583 us -> 579 us (level)
  no operation moved by 1% of the time
where the time goes in v3:
time: 579 us; the launch traced here: 578 us
  Pallas kernels  533 us (92%)
  starting transfers between devices  38.9 us (7%)
    pallas_call x1, Pallas kernels, exchange(): pl.pallas_call(functools.partial(kernel, n, m), out_shape=(jax.ShapeDtype...  514 us
    ppermute x1, starting transfers between devices, body(): got = lax.ppermute(tail, 'fsdp', [(i, (i + n // 2) % n) for i in range(n)])  38.9 us
    pallas_call x1, Pallas kernels, settle(): pl.pallas_call(settle_kernel, out_shape=tuple((jax.ShapeDtypeStruct(a.sha...  18.1 us
  transfers between devices with their start and end apart: 1, of which 1 were waited for; matrix products, arithmetic and copies ran while one was open for 0% of the time, Pallas kernels for 3%

profile of v3, /device:TPU:0, one launch (start us, length us, event | category | flops | bytes accessed | tf_op | source)
XLA Modules:
  0.0 578.3 jit_solution(3771498264614030526)
XLA Ops:
  0.6 514.4 %shard_map.58 = (bf16[4,800,4096]{2,1,0:T(8,128)(2,1)}, f32[4,800]{1,0:T(4,128)}, bf16[16,4096]{1,0:T(8,128)(2,1)}, bf16[544,512]{1,0:T(8,128)(2,1)}) custom-call(f32[4,6400,512]{2,1,0:T(8,128)} %w.1, f32[4,512]{1,0:T(4,128)} %bitcast.3, f32[1,512]{1,0:T(1,128)} %bitcast.4), custom_call_target="tpu_custom_call" | custom-call | tf_op jit(solution)/shard_map/pallas_call | solution.py:489
  515.0 38.9 %collective-permute-start = (bf16[544,512]{1,0:T(8,128)(2,1)}, bf16[544,512]{1,0:T(8,128)(2,1)S(1)}, u32[]{:S(2)}, u32[]{:S(2)}) collective-permute-start(bf16[544,512]{1,0:T(8,128)(2,1)} %get-tuple-element.14), channel_id=1, source_target_pairs={{0,4},{1,5},{2,6},{3,7},{4,0},{5,1},{6,2},{7,3},{8,12},{9,13},{10,... | collective-permute-start | bytes 1671176 | tf_op jit(solution)/shard_map/ppermute | solution.py:600
  553.9 0.0 copy-start
  553.9 0.9 copy-done
  554.8 0.0 copy-start.1
  554.8 0.7 copy-done.1
  555.5 18.1 %shard_map.59 = (bf16[4,800,4096]{2,1,0:T(8,128)(2,1)}, f32[4,800]{1,0:T(4,128)}, bf16[16,4096]{1,0:T(8,128)(2,1)}) custom-call(bf16[4,800,4096]{2,1,0:T(8,128)(2,1)} %get-tuple-element.10.o, f32[4,800]{1,0:T(4,128)S(1)} %copy-done.1, bf16[16,4096]{1,0:T(8,128)(2,1)S(1)} %copy-done), custom_call_target="tpu_custom_call" | custom-call | bytes 52428800 | tf_op jit(solution)/shard_map/pallas_call | solution.py:562
  573.6 3.9 collective-permute-done.got
  577.5 0.8 shard_map.60
Async XLA Ops:
  515.0 62.5 %collective-permute-start = (bf16[544,512]{1,0:T(8,128)(2,1)}, bf16[544,512]{1,0:T(8,128)(2,1)S(1)}, u32[]{:S(2)}, u32[]{:S(2)}) collective-permute-start(bf16[544,512]{1,0:T(8,128)(2,1)} %get-tuple-element.14), channel_id=1, source_target_pairs={{0,4},{1,5},{2,6},{3,7},{4,0},{5,1},{6,2},{7,3},{8,12},{9,13},{10,... | collective-permute-start | bytes 1671176 | tf_op jit(solution)/shard_map/ppermute | solution.py:600
  553.9 0.9 copy-start
  554.8 0.7 copy-start.1

commit v4 on v3

--- a/solution.py
+++ b/solution.py
@@ -10,7 +10,7 @@
 LANES = 128
 TAIL_START = 32
 LEADS = 2
-CUTS = (64, 96, 128, 160)
+CUTS = (80, 128, 176, 224)
 VMEM_BYTES = 67043328
 MESH = pl.DeviceIdType.MESH
 

time: 579 us -> 579 us (level)
  no operation moved by 1% of the time
where the time goes in v4:
time: 579 us; the launch traced here: 578 us
  Pallas kernels  533 us (92%)
  starting transfers between devices  38.3 us (7%)
    pallas_call x1, Pallas kernels, exchange(): pl.pallas_call(functools.partial(kernel, n, m), out_shape=(jax.ShapeDtype...  514 us
    ppermute x1, starting transfers between devices, body(): got = lax.ppermute(tail, 'fsdp', [(i, (i + n // 2) % n) for i in range(n)])  38.3 us
    pallas_call x1, Pallas kernels, settle(): pl.pallas_call(settle_kernel, out_shape=tuple((jax.ShapeDtypeStruct(a.sha...  18.1 us
  transfers between devices with their start and end apart: 1, of which 1 were waited for; matrix products, arithmetic and copies ran while one was open for 0% of the time, Pallas kernels for 3%

profile of v4, /device:TPU:0, one launch (start us, length us, event | category | flops | bytes accessed | tf_op | source)
XLA Modules:
  0.0 578.3 jit_solution(8166230184866788314)
XLA Ops:
  0.6 514.4 %shard_map.58 = (bf16[4,800,4096]{2,1,0:T(8,128)(2,1)}, f32[4,800]{1,0:T(4,128)}, bf16[16,4096]{1,0:T(8,128)(2,1)}, bf16[544,512]{1,0:T(8,128)(2,1)}) custom-call(f32[4,6400,512]{2,1,0:T(8,128)} %w.1, f32[4,512]{1,0:T(4,128)} %bitcast.3, f32[1,512]{1,0:T(1,128)} %bitcast.4), custom_call_target="tpu_custom_call" | custom-call | tf_op jit(solution)/shard_map/pallas_call | solution.py:489
  515.1 38.3 %collective-permute-start = (bf16[544,512]{1,0:T(8,128)(2,1)}, bf16[544,512]{1,0:T(8,128)(2,1)S(1)}, u32[]{:S(2)}, u32[]{:S(2)}) collective-permute-start(bf16[544,512]{1,0:T(8,128)(2,1)} %get-tuple-element.14), channel_id=1, source_target_pairs={{0,4},{1,5},{2,6},{3,7},{4,0},{5,1},{6,2},{7,3},{8,12},{9,13},{10,... | collective-permute-start | bytes 1671176 | tf_op jit(solution)/shard_map/ppermute | solution.py:600
  553.3 0.0 copy-start
  553.3 0.9 copy-done
  554.2 0.0 copy-start.1
  554.2 0.7 copy-done.1
  554.9 18.1 %shard_map.59 = (bf16[4,800,4096]{2,1,0:T(8,128)(2,1)}, f32[4,800]{1,0:T(4,128)}, bf16[16,4096]{1,0:T(8,128)(2,1)}) custom-call(bf16[4,800,4096]{2,1,0:T(8,128)(2,1)} %get-tuple-element.10.o, f32[4,800]{1,0:T(4,128)S(1)} %copy-done.1, bf16[16,4096]{1,0:T(8,128)(2,1)S(1)} %copy-done), custom_call_target="tpu_custom_call" | custom-call | bytes 52428800 | tf_op jit(solution)/shard_map/pallas_call | solution.py:562
  573.0 4.4 collective-permute-done.got
  577.5 0.8 shard_map.60
Async XLA Ops:
  515.1 62.4 %collective-permute-start = (bf16[544,512]{1,0:T(8,128)(2,1)}, bf16[544,512]{1,0:T(8,128)(2,1)S(1)}, u32[]{:S(2)}, u32[]{:S(2)}) collective-permute-start(bf16[544,512]{1,0:T(8,128)(2,1)} %get-tuple-element.14), channel_id=1, source_target_pairs={{0,4},{1,5},{2,6},{3,7},{4,0},{5,1},{6,2},{7,3},{8,12},{9,13},{10,... | collective-permute-start | bytes 1671176 | tf_op jit(solution)/shard_map/ppermute | solution.py:600
  553.3 0.9 copy-start
  554.2 0.7 copy-start.1
